TPU v7x, 256 devices: a whole 4x4x8 slice. The times are simulated.
256 devices in a mesh: rep: 2 (over core), dp: 128 (over x, y, z).
Axes of the slice: x: 4, y: 4, z: 8, core: 2. Of those that a mesh axis runs over, the one named last changes fastest.
Arguments:
- a: bfloat16 [256, 2, 4096, 768], P(('rep', 'dp')), parts along dimension 0
- g: bfloat16 [256, 2, 4096, 1792], P(('rep', 'dp')), parts along dimension 0
Outputs:
- output: bfloat16 [4, 768, 1792], P('rep'), parts along dimension 0
There are 2 independent parts. A program takes and returns all parts, laid end to end along the dimension named above; each array names one.
All inputs are finite; a program needn't handle non-finite values.
Results may differ from a plain program's by a relative error of at most 0.012.
Values are sent between devices in bfloat16 or wider.
A program may use at most 768 MiB of HBM per device.

v0:
```python
import jax
import jax.numpy as jnp
from jax import lax
from jax.experimental import pallas as pl
from jax.experimental.pallas import tpu as pltpu
from jax.sharding import PartitionSpec as P

X, Y, Z = 4, 4, 8
U, L = 48, 128
UNITS = 32
W = 2 * L
AFTER = (0, 3, 5, 7, 9, 12, 15, 17, 21, 26)
ORDER = (3, 2, 8, 1, 6, 5, 4, 9, 7)
GBUF = 4
MB = 384
bf16, f32 = jnp.bfloat16, jnp.float32


def kernel(a_hbm, g_hbm, outb, abuf, gbuf, term, recv1, acc, part, recv2, exch,
           asem, gsem, ssem, r1sem, r2sem, xsem, g2sem, g1sem):
    mats, tokens, d = a_hbm.shape
    per = g_hbm.shape[2] // W
    pieces = mats * per
    me = lax.axis_index("dp")
    x, y, z = me // (Y * Z), (me // Z) % Y, me % Z

    def load_a(n):
        return pltpu.make_async_copy(a_hbm.at[n], abuf.at[n], asem.at[n])

    def load_g(t):
        col = pl.multiple_of((t % per) * W, W)
        slot = t % GBUF
        return pltpu.make_async_copy(g_hbm.at[t // per, :, pl.ds(col, W)], gbuf.at[slot], gsem.at[slot])

    def compute(t):
        n, slot = t // per, t % GBUF
        load_g(t).wait()

        @pl.when(t % per == 0)
        def _():
            load_a(n).wait()

        for m in range(0, d, MB):
            s = lax.dot_general(abuf[n, :, m : m + MB], gbuf[slot], (((0,), (0,)), ((), ())), preferred_element_type=f32).astype(bf16)
            for h in range(2):
                u = h * (UNITS // 2) + m // U
                term[t, u : u + MB // U] = s[:, h * L : (h + 1) * L].reshape(MB // U, U, L)

    def place(p):
        odd = p % 2
        s = 1 - 2 * ((p // 2) % 2)
        c1, st1 = x + odd * (y - x), Y * Z - odd * (Y * Z - Z)
        c3, st3 = y + odd * (x - y), Z + odd * (Y * Z - Z)

        def on1(k):
            return (c1 + k + 8) % 4

        def on3(k):
            return (c3 + k + 8) % 4

        def onz(k):
            return (z + k + 8) % 8

        dev1 = lambda k: me + (on1(k) - c1) * st1
        dev3 = lambda k: me + (on3(k) - c3) * st3
        devz = lambda k: me + onz(k) - z
        return s, c1, c3, on1, on3, onz, dev1, dev3, devz

    def send(src, dst, p, sem, dev):
        pltpu.make_async_remote_copy(
            src_ref=src, dst_ref=dst, send_sem=ssem.at[p], recv_sem=sem,
            device_id={"dp": dev}, device_id_type=pl.DeviceIdType.MESH,
        ).start()

    def wait(ref, sem):
        pltpu.make_async_copy(ref, ref, sem).wait()

    def chunk(c):
        return pl.ds(c * Z, Z)

    def half(c, h):
        return pl.ds(c * Z + h * (Z // 2), Z // 2)

    def step0(p):
        s, c1, c3, on1, on3, onz, dev1, dev3, devz = place(p)
        for h, o in ((0, 1), (1, -1)):
            send(term.at[p, half(on1(2), h)], recv1.at[p, h], p, r1sem.at[p, h], dev1(-o))
        for h, o in ((0, 1), (1, -1)):
            send(term.at[p, half(on1(o), h)], recv1.at[p, 2 + h], p, r1sem.at[p, 2 + h], dev1(o))

    def step1(p):
        s, c1, c3, on1, on3, onz, dev1, dev3, devz = place(p)
        for h, o in ((0, 1), (1, -1)):
            wait(recv1.at[p, h], r1sem.at[p, h])
            base = on1(-o) * Z + h * (Z // 2)
            for u in range(Z // 2):
                term[p, base + u] = (term[p, base + u].astype(f32) + recv1[p, h, u].astype(f32)).astype(bf16)
            send(term.at[p, half(on1(-o), h)], recv1.at[p, 4 + h], p, r1sem.at[p, 4 + h], dev1(-o))

    def step2(p):
        s, c1, c3, on1, on3, onz, dev1, dev3, devz = place(p)
        for k in range(2, 6):
            wait(recv1.at[p, k], r1sem.at[p, k])
        for u in range(Z):
            h, w = divmod(u, Z // 2)
            v = term[p, c1 * Z + u].astype(f32) + recv1[p, 2 + h, w].astype(f32) + recv1[p, 4 + h, w].astype(f32)
            acc[p, u] = v
            part[p, u] = v.astype(bf16)
        send(part.at[p, onz(4)], recv2.at[p, 0], p, r2sem.at[p, 0], devz(-2 * s))
        send(part.at[p, onz(-3 * s)], recv2.at[p, 1], p, r2sem.at[p, 1], devz(-s))
        send(part.at[p, onz(3 * s)], recv2.at[p, 2], p, r2sem.at[p, 2], devz(s))
        send(part.at[p, onz(-s)], recv2.at[p, 3], p, r2sem.at[p, 3], devz(-s))
        send(part.at[p, onz(s)], recv2.at[p, 4], p, r2sem.at[p, 4], devz(s))

    def step3(p):
        s, c1, c3, on1, on3, onz, dev1, dev3, devz = place(p)
        for k in range(3):
            wait(recv2.at[p, k], r2sem.at[p, k])
        far, near = onz(-2 * s), onz(2 * s)
        part[p, far] = (acc[p, far] + recv2[p, 0].astype(f32) + recv2[p, 1].astype(f32)).astype(bf16)
        part[p, near] = (acc[p, near] + recv2[p, 2].astype(f32)).astype(bf16)
        send(part.at[p, far], recv2.at[p, 5], p, r2sem.at[p, 5], devz(-2 * s))
        send(part.at[p, near], recv2.at[p, 6], p, r2sem.at[p, 6], devz(2 * s))

    def step4(p):
        s, c1, c3, on1, on3, onz, dev1, dev3, devz = place(p)
        for k in range(3, 7):
            wait(recv2.at[p, k], r2sem.at[p, k])
        v = acc[p, z]
        for k in range(3, 7):
            v = v + recv2[p, k].astype(f32)
        exch[p, c3] = v.astype(bf16)
        for k in range(1, 4):
            send(exch.at[p, c3], exch.at[p, c3], p, xsem.at[p, k - 1], dev3(k))

    def step5(p):
        s, c1, c3, on1, on3, onz, dev1, dev3, devz = place(p)
        for k in range(1, 4):
            wait(exch.at[p, on3(-k)], xsem.at[p, k - 1])
        v = exch[p, 0].astype(f32)
        for k in range(1, 4):
            v = v + exch[p, k].astype(f32)
        u = c1 * Z + z
        outb[p, u] = v.astype(bf16)
        for k, h in enumerate((-2, 2, -1, 1)):
            send(outb.at[p, u], outb.at[p, u], p, g2sem.at[p, k], devz(h * s))

    def step6(p):
        s, c1, c3, on1, on3, onz, dev1, dev3, devz = place(p)
        far, near = c1 * Z + onz(2 * s), c1 * Z + onz(-2 * s)
        wait(outb.at[p, far], g2sem.at[p, 0])
        send(outb.at[p, far], outb.at[p, far], p, g2sem.at[p, 4], devz(-2 * s))
        send(outb.at[p, far], outb.at[p, far], p, g2sem.at[p, 5], devz(-s))
        wait(outb.at[p, near], g2sem.at[p, 1])
        send(outb.at[p, near], outb.at[p, near], p, g2sem.at[p, 6], devz(s))

    def step7(p):
        s, c1, c3, on1, on3, onz, dev1, dev3, devz = place(p)
        for k, h in ((2, 1), (3, -1), (4, 4), (5, 3), (6, -3)):
            wait(outb.at[p, c1 * Z + onz(h * s)], g2sem.at[p, k])
        mine = outb.at[p, chunk(c1)]
        for h, o in ((0, 1), (1, -1)):
            send(mine, mine, p, g1sem.at[p, h], dev1(-o))

    def step8(p):
        s, c1, c3, on1, on3, onz, dev1, dev3, devz = place(p)
        for h, o in ((0, 1), (1, -1)):
            wait(outb.at[p, chunk(on1(o))], g1sem.at[p, h])
            one = outb.at[p, half(on1(o), h)]
            send(one, one, p, g1sem.at[p, 2 + h], dev1(-o))

    def step9(p):
        s, c1, c3, on1, on3, onz, dev1, dev3, devz = place(p)
        for h in range(2):
            wait(outb.at[p, half(on1(2), h)], g1sem.at[p, 2 + h])

    steps = [step0, step1, step2, step3, step4, step5, step6, step7, step8, step9]

    load_a(0).start()
    for t in range(GBUF - 1):
        load_g(t).start()
    for n in range(1, mats):
        load_a(n).start()

    barrier = pltpu.get_barrier_semaphore()
    _, _, _, _, _, _, devx, devy, devz = place(0)
    partners = [devx(k) for k in (1, 2, 3)] + [devy(k) for k in (1, 2, 3)] + [devz(k) for k in (-2, -1, 1, 2)]
    for dev in partners:
        pl.semaphore_signal(barrier, inc=1, device_id={"dp": dev}, device_id_type=pl.DeviceIdType.MESH)

    pl.semaphore_wait(barrier, len(partners))

    @pl.loop(0, pieces + AFTER[-1])
    def _(t):
        @pl.when(t < pieces)
        def _():
            @pl.when(t + GBUF - 1 < pieces)
            def _():
                load_g(t + GBUF - 1).start()

            compute(t)
            step0(t)

        for k in ORDER:
            p = t - AFTER[k]

            @pl.when((p >= 0) & (p < pieces))
            def _():
                steps[k](p)

    @pl.loop(0, pieces)
    def _(p):
        wait(sent_bytes(term), ssem.at[p])


def sent_bytes(term):
    return term.at[pl.ds(0, 5), pl.ds(0, 13)]


def store(panels, out_hbm, sem):
    pieces = panels.shape[0]
    per = pieces // out_hbm.shape[0]
    copies = []
    for p in range(pieces):
        for h in range(2):
            col = (p % per) * W + h * L
            src, dst = panels.at[p, pl.ds(h * (UNITS // 2), UNITS // 2)], out_hbm.at[p // per, :, :, pl.ds(col, L)]
            copies.append(pltpu.make_async_copy(src, dst, sem.at[p, h]))
    for copy in copies:
        copy.start()
    for copy in copies:
        copy.wait()


def solution(mesh):
    assert mesh.shape["dp"] == X * Y * Z

    def body(a, g):
        _, mats, tokens, d = a.shape
        ff = g.shape[3]
        pieces = mats * ff // W
        vmem = lambda *shape, dtype=bf16: pltpu.VMEM(shape, dtype)
        dma = pltpu.SemaphoreType.DMA
        panels = pl.pallas_call(
            kernel,
            name="wgrad_sums",
            out_shape=pltpu.VMEM((pieces, UNITS, U, L), bf16),
            in_specs=[pl.BlockSpec(memory_space=pl.ANY)] * 2,
            out_specs=pl.BlockSpec(memory_space=pltpu.VMEM),
            scratch_shapes=[
                vmem(mats, tokens, d),
                vmem(GBUF, tokens, W),
                vmem(pieces, UNITS, U, L),
                vmem(pieces, 6, Z // 2, U, L),
                vmem(pieces, Z, U, L, dtype=f32),
                vmem(pieces, Z, U, L),
                vmem(pieces, 7, U, L),
                vmem(pieces, 4, U, L),
                dma((mats,)),
                dma((GBUF,)),
                dma((pieces,)),
                dma((pieces, 6)),
                dma((pieces, 7)),
                dma((pieces, 3)),
                dma((pieces, 7)),
                dma((pieces, 4)),
            ],
            compiler_params=pltpu.CompilerParams(has_side_effects=True, collective_id=0, vmem_limit_bytes=50 << 20),
        )(a[0], g[0])
        out = pl.pallas_call(
            store,
            name="store_sums",
            out_shape=jax.ShapeDtypeStruct((mats, d // U, U, ff), bf16),
            in_specs=[pl.BlockSpec(memory_space=pltpu.VMEM)],
            out_specs=pl.BlockSpec(memory_space=pl.ANY),
            scratch_shapes=[dma((pieces, 2))],
            compiler_params=pltpu.CompilerParams(vmem_limit_bytes=8 << 20),
        )(panels)
        return out.reshape(mats, d, ff)

    return jax.shard_map(body, mesh=mesh, in_specs=(P(("rep", "dp")),) * 2, out_specs=P("rep"), check_vma=False)
```

profile of v0, /device:TPU:8, one launch (start us, length us, event | category | flops | bytes accessed | tf_op | source)
XLA Modules:
  0.0 86.1 jit_solution(12978088413036840506)
XLA Ops:
  0.0 83.5 %wgrad_sums.1.panels = bf16[14,32,48,128]{3,2,1,0:T(8,128)(2,1)S(1)} custom-call(bf16[2,4096,768]{2,1,0:T(8,128)(2,1)} %bitcast.4, bf16[2,4096,1792]{2,1,0:T(8,128)(2,1)} %bitcast.3), custom_call_target="tpu_custom_call" | custom-call | tf_op jit(solution)/shard_map/wgrad_sums/pallas_call | solution.py:244
  83.5 2.6 %store_sums.1 = bf16[2,16,48,1792]{3,2,1,0:T(8,128)(2,1)} custom-call(bf16[14,32,48,128]{3,2,1,0:T(8,128)(2,1)S(1)} %wgrad_sums.1.panels), custom_call_target="tpu_custom_call" | custom-call | tf_op jit(solution)/shard_map/store_sums/pallas_call | solution.py:270
where the time goes:
time: 86.3 us; the launch traced here: 86.1 us
  Pallas kernels  86.1 us (100%)
    pallas_call x1, Pallas kernels, body(): pl.pallas_call(kernel, name='wgrad_sums', out_shape=pltpu.VMEM((pieces, U...  83.5 us
    pallas_call x1, Pallas kernels, body(): pl.pallas_call(store, name='store_sums', out_shape=jax.ShapeDtypeStruct((...  2.64 us

commit v1 on v0

--- a/solution.py
+++ b/solution.py
@@ -40,6 +40,21 @@
         def _():
             load_a(n).wait()
 
+        @pl.when(t == 0)
+        def _():
+            for k in range(1, GBUF - 1):
+                load_g(k).start()
+
+        @pl.when(t + GBUF - 1 < pieces)
+        def _():
+            load_g(t + GBUF - 1).start()
+
+        @pl.when(t % per == 1)
+        def _():
+            @pl.when(n + 1 < mats)
+            def _():
+                load_a(n + 1).start()
+
         for m in range(0, d, MB):
             s = lax.dot_general(abuf[n, :, m : m + MB], gbuf[slot], (((0,), (0,)), ((), ())), preferred_element_type=f32).astype(bf16)
             for h in range(2):
@@ -86,7 +101,7 @@
         for h, o in ((0, 1), (1, -1)):
             send(term.at[p, half(on1(2), h)], recv1.at[p, h], p, r1sem.at[p, h], dev1(-o))
         for h, o in ((0, 1), (1, -1)):
-            send(term.at[p, half(on1(o), h)], recv1.at[p, 2 + h], p, r1sem.at[p, 2 + h], dev1(o))
+            send(term.at[p, half(on1(o), h)], recv1.at[p, 2 + h], p, r1sem.at[p, 2], dev1(o))
 
     def step1(p):
         s, c1, c3, on1, on3, onz, dev1, dev3, devz = place(p)
@@ -95,92 +110,82 @@
             base = on1(-o) * Z + h * (Z // 2)
             for u in range(Z // 2):
                 term[p, base + u] = (term[p, base + u].astype(f32) + recv1[p, h, u].astype(f32)).astype(bf16)
-            send(term.at[p, half(on1(-o), h)], recv1.at[p, 4 + h], p, r1sem.at[p, 4 + h], dev1(-o))
+            send(term.at[p, half(on1(-o), h)], recv1.at[p, 4 + h], p, r1sem.at[p, 2], dev1(-o))
 
     def step2(p):
         s, c1, c3, on1, on3, onz, dev1, dev3, devz = place(p)
-        for k in range(2, 6):
-            wait(recv1.at[p, k], r1sem.at[p, k])
+        wait(recv1.at[p, pl.ds(2, 4)], r1sem.at[p, 2])
         for u in range(Z):
             h, w = divmod(u, Z // 2)
             v = term[p, c1 * Z + u].astype(f32) + recv1[p, 2 + h, w].astype(f32) + recv1[p, 4 + h, w].astype(f32)
             acc[p, u] = v
             part[p, u] = v.astype(bf16)
         send(part.at[p, onz(4)], recv2.at[p, 0], p, r2sem.at[p, 0], devz(-2 * s))
-        send(part.at[p, onz(-3 * s)], recv2.at[p, 1], p, r2sem.at[p, 1], devz(-s))
-        send(part.at[p, onz(3 * s)], recv2.at[p, 2], p, r2sem.at[p, 2], devz(s))
-        send(part.at[p, onz(-s)], recv2.at[p, 3], p, r2sem.at[p, 3], devz(-s))
-        send(part.at[p, onz(s)], recv2.at[p, 4], p, r2sem.at[p, 4], devz(s))
+        send(part.at[p, onz(-3 * s)], recv2.at[p, 1], p, r2sem.at[p, 0], devz(-s))
+        send(part.at[p, onz(3 * s)], recv2.at[p, 2], p, r2sem.at[p, 0], devz(s))
+        send(part.at[p, onz(-s)], recv2.at[p, 3], p, r2sem.at[p, 1], devz(-s))
+        send(part.at[p, onz(s)], recv2.at[p, 4], p, r2sem.at[p, 1], devz(s))
 
     def step3(p):
         s, c1, c3, on1, on3, onz, dev1, dev3, devz = place(p)
-        for k in range(3):
-            wait(recv2.at[p, k], r2sem.at[p, k])
+        wait(recv2.at[p, pl.ds(0, 3)], r2sem.at[p, 0])
         far, near = onz(-2 * s), onz(2 * s)
         part[p, far] = (acc[p, far] + recv2[p, 0].astype(f32) + recv2[p, 1].astype(f32)).astype(bf16)
         part[p, near] = (acc[p, near] + recv2[p, 2].astype(f32)).astype(bf16)
-        send(part.at[p, far], recv2.at[p, 5], p, r2sem.at[p, 5], devz(-2 * s))
-        send(part.at[p, near], recv2.at[p, 6], p, r2sem.at[p, 6], devz(2 * s))
+        send(part.at[p, far], recv2.at[p, 5], p, r2sem.at[p, 1], devz(-2 * s))
+        send(part.at[p, near], recv2.at[p, 6], p, r2sem.at[p, 1], devz(2 * s))
 
     def step4(p):
         s, c1, c3, on1, on3, onz, dev1, dev3, devz = place(p)
-        for k in range(3, 7):
-            wait(recv2.at[p, k], r2sem.at[p, k])
+        wait(recv2.at[p, pl.ds(3, 4)], r2sem.at[p, 1])
         v = acc[p, z]
         for k in range(3, 7):
             v = v + recv2[p, k].astype(f32)
         exch[p, c3] = v.astype(bf16)
         for k in range(1, 4):
-            send(exch.at[p, c3], exch.at[p, c3], p, xsem.at[p, k - 1], dev3(k))
+            send(exch.at[p, c3], exch.at[p, c3], p, xsem.at[p], dev3(k))
 
     def step5(p):
         s, c1, c3, on1, on3, onz, dev1, dev3, devz = place(p)
-        for k in range(1, 4):
-            wait(exch.at[p, on3(-k)], xsem.at[p, k - 1])
+        wait(exch.at[p, pl.ds(0, 3)], xsem.at[p])
         v = exch[p, 0].astype(f32)
         for k in range(1, 4):
             v = v + exch[p, k].astype(f32)
         u = c1 * Z + z
         outb[p, u] = v.astype(bf16)
-        for k, h in enumerate((-2, 2, -1, 1)):
-            send(outb.at[p, u], outb.at[p, u], p, g2sem.at[p, k], devz(h * s))
+        for h in (-2, 2, -1, 1):
+            send(outb.at[p, u], outb.at[p, u], p, g2sem.at[p, 0 if h in (-2, 2) else 1], devz(h * s))
 
     def step6(p):
         s, c1, c3, on1, on3, onz, dev1, dev3, devz = place(p)
         far, near = c1 * Z + onz(2 * s), c1 * Z + onz(-2 * s)
-        wait(outb.at[p, far], g2sem.at[p, 0])
-        send(outb.at[p, far], outb.at[p, far], p, g2sem.at[p, 4], devz(-2 * s))
-        send(outb.at[p, far], outb.at[p, far], p, g2sem.at[p, 5], devz(-s))
-        wait(outb.at[p, near], g2sem.at[p, 1])
-        send(outb.at[p, near], outb.at[p, near], p, g2sem.at[p, 6], devz(s))
+        wait(outb.at[p, pl.ds(0, 2)], g2sem.at[p, 0])
+        send(outb.at[p, far], outb.at[p, far], p, g2sem.at[p, 1], devz(-2 * s))
+        send(outb.at[p, far], outb.at[p, far], p, g2sem.at[p, 1], devz(-s))
+        send(outb.at[p, near], outb.at[p, near], p, g2sem.at[p, 1], devz(s))
 
     def step7(p):
         s, c1, c3, on1, on3, onz, dev1, dev3, devz = place(p)
-        for k, h in ((2, 1), (3, -1), (4, 4), (5, 3), (6, -3)):
-            wait(outb.at[p, c1 * Z + onz(h * s)], g2sem.at[p, k])
-        mine = outb.at[p, chunk(c1)]
-        for h, o in ((0, 1), (1, -1)):
-            send(mine, mine, p, g1sem.at[p, h], dev1(-o))
+        wait(outb.at[p, pl.ds(0, 5)], g2sem.at[p, 1])
+        for w in range(2):
+            for h, o in ((0, 1), (1, -1)):
+                mine = outb.at[p, half(c1, h)]
+                send(mine, mine, p, g1sem.at[p, w], dev1(o * (2 * w - 1)))
 
     def step8(p):
         s, c1, c3, on1, on3, onz, dev1, dev3, devz = place(p)
-        for h, o in ((0, 1), (1, -1)):
-            wait(outb.at[p, chunk(on1(o))], g1sem.at[p, h])
+        wait(outb.at[p, chunk(0)], g1sem.at[p, 0])
+        for h, o in ((0, 1), (1, -1)):
             one = outb.at[p, half(on1(o), h)]
-            send(one, one, p, g1sem.at[p, 2 + h], dev1(-o))
+            send(one, one, p, g1sem.at[p, 1], dev1(-o))
 
     def step9(p):
-        s, c1, c3, on1, on3, onz, dev1, dev3, devz = place(p)
-        for h in range(2):
-            wait(outb.at[p, half(on1(2), h)], g1sem.at[p, 2 + h])
+        wait(outb.at[p, pl.ds(0, 2 * Z)], g1sem.at[p, 1])
 
     steps = [step0, step1, step2, step3, step4, step5, step6, step7, step8, step9]
 
     load_a(0).start()
-    for t in range(GBUF - 1):
-        load_g(t).start()
-    for n in range(1, mats):
-        load_a(n).start()
+    load_g(0).start()
 
     barrier = pltpu.get_barrier_semaphore()
     _, _, _, _, _, _, devx, devy, devz = place(0)
@@ -194,10 +199,6 @@
     def _(t):
         @pl.when(t < pieces)
         def _():
-            @pl.when(t + GBUF - 1 < pieces)
-            def _():
-                load_g(t + GBUF - 1).start()
-
             compute(t)
             step0(t)
 
@@ -259,11 +260,11 @@
                 dma((mats,)),
                 dma((GBUF,)),
                 dma((pieces,)),
-                dma((pieces, 6)),
-                dma((pieces, 7)),
                 dma((pieces, 3)),
-                dma((pieces, 7)),
-                dma((pieces, 4)),
+                dma((pieces, 2)),
+                dma((pieces,)),
+                dma((pieces, 2)),
+                dma((pieces, 2)),
             ],
             compiler_params=pltpu.CompilerParams(has_side_effects=True, collective_id=0, vmem_limit_bytes=50 << 20),
         )(a[0], g[0])

time: 86.3 us -> 83.4 us (0.966)
  Pallas kernels: 86.1 us -> 83.3 us
    pallas_call x1, Pallas kernels: 83.5 us -> 80.6 us  [body(): pl.pallas_call(kernel, name='wgrad_sums', out_shape=pltpu.VMEM((pieces, U...]
where the time goes in v1:
time: 83.4 us; the launch traced here: 83.3 us
  Pallas kernels  83.3 us (100%)
    pallas_call x1, Pallas kernels, body(): pl.pallas_call(kernel, name='wgrad_sums', out_shape=pltpu.VMEM((pieces, U...  80.6 us
    pallas_call x1, Pallas kernels, body(): pl.pallas_call(store, name='store_sums', out_shape=jax.ShapeDtypeStruct((...  2.64 us

profile of v1, /device:TPU:8, one launch (start us, length us, event | category | flops | bytes accessed | tf_op | source)
XLA Modules:
  0.0 83.3 jit_solution(12911607863045979857)
XLA Ops:
  0.0 80.6 %wgrad_sums.1.panels = bf16[14,32,48,128]{3,2,1,0:T(8,128)(2,1)S(1)} custom-call(bf16[2,4096,768]{2,1,0:T(8,128)(2,1)} %bitcast.4, bf16[2,4096,1792]{2,1,0:T(8,128)(2,1)} %bitcast.3), custom_call_target="tpu_custom_call" | custom-call | tf_op jit(solution)/shard_map/wgrad_sums/pallas_call | solution.py:245
  80.6 2.6 %store_sums.1 = bf16[2,16,48,1792]{3,2,1,0:T(8,128)(2,1)} custom-call(bf16[14,32,48,128]{3,2,1,0:T(8,128)(2,1)S(1)} %wgrad_sums.1.panels), custom_call_target="tpu_custom_call" | custom-call | tf_op jit(solution)/shard_map/store_sums/pallas_call | solution.py:271

commit v2 on v1

--- a/solution.py
+++ b/solution.py
@@ -9,8 +9,8 @@
 U, L = 48, 128
 UNITS = 32
 W = 2 * L
-AFTER = (0, 3, 5, 7, 9, 12, 15, 17, 21, 26)
-ORDER = (3, 2, 8, 1, 6, 5, 4, 9, 7)
+AFTER = (0, 3, 5, 7, 9, 12, 15, 17, 20, 25)
+ORDER = (3, 2, 9, 1, 6, 5, 4, 8, 7)
 GBUF = 4
 MB = 384
 bf16, f32 = jnp.bfloat16, jnp.float32
@@ -142,7 +142,7 @@
         for k in range(3, 7):
             v = v + recv2[p, k].astype(f32)
         exch[p, c3] = v.astype(bf16)
-        for k in range(1, 4):
+        for k in (2, 1, 3):
             send(exch.at[p, c3], exch.at[p, c3], p, xsem.at[p], dev3(k))
 
     def step5(p):

time: 83.4 us -> 83.6 us (level)
  no operation moved by 1% of the time
where the time goes in v2:
time: 83.6 us; the launch traced here: 83.4 us
  Pallas kernels  83.4 us (100%)
    pallas_call x1, Pallas kernels, body(): pl.pallas_call(kernel, name='wgrad_sums', out_shape=pltpu.VMEM((pieces, U...  80.7 us
    pallas_call x1, Pallas kernels, body(): pl.pallas_call(store, name='store_sums', out_shape=jax.ShapeDtypeStruct((...  2.64 us

profile of v2, /device:TPU:8, one launch (start us, length us, event | category | flops | bytes accessed | tf_op | source)
XLA Modules:
  0.0 83.4 jit_solution(15658988260920321704)
XLA Ops:
  0.0 80.7 %wgrad_sums.1.panels = bf16[14,32,48,128]{3,2,1,0:T(8,128)(2,1)S(1)} custom-call(bf16[2,4096,768]{2,1,0:T(8,128)(2,1)} %bitcast.4, bf16[2,4096,1792]{2,1,0:T(8,128)(2,1)} %bitcast.3), custom_call_target="tpu_custom_call" | custom-call | tf_op jit(solution)/shard_map/wgrad_sums/pallas_call | solution.py:245
  80.7 2.6 %store_sums.1 = bf16[2,16,48,1792]{3,2,1,0:T(8,128)(2,1)} custom-call(bf16[14,32,48,128]{3,2,1,0:T(8,128)(2,1)S(1)} %wgrad_sums.1.panels), custom_call_target="tpu_custom_call" | custom-call | tf_op jit(solution)/shard_map/store_sums/pallas_call | solution.py:271
